TPU v7x, 32 devices: a whole 2x2x4 slice. The times are simulated.
32 devices in a mesh: fsdp: 32 (over z, y, x, core), dp: 1.
Axes of the slice: x: 2, y: 2, z: 4, core: 2. Of those that a mesh axis runs over, the one named last changes fastest.
Arguments:
- inputs: bfloat16 [8192, 2560], P(('fsdp', 'dp')), may hold values from -6 to 6
- value_cotangent: bfloat16 [8192, 512], P(('fsdp', 'dp')), may hold values from -0.15625 to 0.15625
- master: float32 [2560, 4, 128], P('fsdp', None, 'dp'), may hold values from -0.125 to 0.125
- first_moment: float32 [2560, 4, 128], P('fsdp', None, 'dp'), may hold values from -6 to 6
- second_moment: float32 [2560, 4, 128], P('fsdp', None, 'dp'), may hold values from 0.25 to 4
Outputs:
- moment_one_new: float32 [2560, 4, 128], P('fsdp', None, 'dp')
- moment_two_new: float32 [2560, 4, 128], P('fsdp', None, 'dp')
- master_new: float32 [2560, 4, 128], P('fsdp', None, 'dp')
- head_blocks: bfloat16 [32, 2560, 128], P('fsdp', None, 'dp')
All inputs are finite; a program needn't handle non-finite values.
Results may differ from a plain program's by a relative error of at most 0.0018.
Values may be sent and summed in bfloat16 or wider, within the bound.
A program may use at most 64 MiB of HBM per device.

v0:
```python
import functools

import jax
import jax.numpy as jnp
from jax import lax
from jax.experimental import pallas as pl
from jax.experimental.pallas import tpu as pltpu
from jax.sharding import PartitionSpec as P

STEP = 8


beta_first = 0.9
beta_second = 0.95
learn_rate = 0.001
weight_decay = 0.1
epsilon = 1e-08


def adam_update(gradient, moment_one, moment_two, weights):
    moment_one_new = beta_first * moment_one + (1.0 - beta_first) * gradient
    moment_two_new = beta_second * moment_two + (1.0 - beta_second) * gradient * gradient
    correct_one = 1.0 - beta_first**STEP
    correct_two = 1.0 - beta_second**STEP
    update = (
        moment_one_new / correct_one / (jnp.sqrt(moment_two_new / correct_two) + epsilon)
        + weight_decay * weights
    )
    return (moment_one_new, moment_two_new, weights - learn_rate * update)


def shards(inputs, value_cotangent, master, first_moment, second_moment):
    _, heads, slice_width = master.shape
    head_size = value_cotangent.shape[1] // heads
    head_parts = []
    for head in range(heads):
        head_cot = value_cotangent[:, head * head_size : (head + 1) * head_size]
        head_term = lax.dot_general(
            inputs, head_cot, (((0,), (0,)), ((), ())), preferred_element_type=jnp.float32
        )
        head_parts.append(
            lax.psum_scatter(
                head_term.astype(jnp.bfloat16), "dp", scatter_dimension=1, tiled=True
            ).astype(jnp.float32)
        )
    column_part = jnp.stack(head_parts, axis=1)
    grad_share = lax.psum_scatter(column_part, "fsdp", scatter_dimension=0, tiled=True)
    moment_one_new, moment_two_new, master_new = adam_update(
        grad_share, first_moment, second_moment, master
    )
    narrow_weight = master_new.astype(jnp.bfloat16)
    gathered = lax.all_gather(narrow_weight, "fsdp", axis=0, tiled=True)
    head_index = lax.axis_index("fsdp") % heads
    picked = lax.dynamic_slice_in_dim(gathered, head_index, 1, 1)
    tp_block = picked.reshape(1, gathered.shape[0], slice_width)
    return (moment_one_new, moment_two_new, master_new, tp_block)


VMEM_BYTES = 67043328
SPARE_BYTES = 64 * 1024
PLANE = 8


def step_kernel(
    n, x_hbm, g_hbm, w_hbm, m_hbm, v_hbm, m_out, v_out, w_out, tp_out,
    x_ref, g_ref, w_ref, m_ref, v_ref,
    mate_x, mate_g, total, parts, plane_in, column_part, column_in, blocks,
    load_sem, mate_send, mate_recv, plane_send, plane_recv,
    column_send, column_recv, line_send, line_recv, row_send, row_recv,
):
    me = lax.axis_index("fsdp")
    z = me // PLANE
    q = lax.rem(me, PLANE)
    spot = q // 2
    core = lax.rem(q, 2)
    mate = me + 1 - 2 * core
    spots = PLANE // 2
    depth = n // PLANE
    layers = depth // 2
    rows, heads, head_size = w_ref.shape
    half = x_ref.shape[1] // 2
    tile = half // layers
    both = 2 * rows
    worker = z // layers

    loads = [
        pltpu.make_async_copy(source, target, load_sem.at[i])
        for i, (source, target) in enumerate(
            ((g_hbm, g_ref), (x_hbm, x_ref), (w_hbm, w_ref), (m_hbm, m_ref), (v_hbm, v_ref))
        )
    ]
    for load in loads:
        load.start()

    def to(device):
        return dict(device_id={"fsdp": device}, device_id_type=pl.DeviceIdType.MESH)

    def plane_mate(step):
        return z * PLANE + lax.rem(q + step, PLANE)

    def layer(step):
        return lax.rem(z + step, depth)

    barrier = pltpu.get_barrier_semaphore()
    for step in range(1, PLANE):
        pl.semaphore_signal(barrier, inc=1, **to(plane_mate(step)))
    for step in range(1, depth):
        for side in range(2):
            pl.semaphore_signal(
                barrier, inc=1, **to(layer(step) * PLANE + 2 * spot + side)
            )
    loads[0].wait()
    loads[1].wait()
    pl.semaphore_wait(barrier, PLANE - 1 + 2 * (depth - 1))

    swap_g = pltpu.make_async_remote_copy(
        g_ref, mate_g, mate_send.at[0], mate_recv.at[0], **to(mate)
    )
    swap_x = [
        pltpu.make_async_remote_copy(
            x_ref.at[:, pl.ds(pl.multiple_of((1 - core) * half + t * tile, 128), tile)],
            mate_x.at[:, pl.ds(t * tile, tile)],
            mate_send.at[1 + t], mate_recv.at[1 + t], **to(mate)
        )
        for t in range(layers)
    ]
    swap_g.start()
    for swap in swap_x:
        swap.start()

    def transposed_dot(left, right):
        return lax.dot_general(
            left, right, (((0,), (0,)), ((), ())), preferred_element_type=jnp.float32
        )

    def rows_of_tile(t):
        return slice(t * tile, (t + 1) * tile)

    for t in range(layers):
        own = x_ref[:, pl.ds(pl.multiple_of(core * half + t * tile, 128), tile)]
        total[rows_of_tile(t), :] = transposed_dot(own, g_ref[...])
    swap_g.wait_recv()

    def plane_copy(phase, t, step, source):
        index = (phase * layers + t) * spots
        target = lax.rem(spot + step, spots)
        return pltpu.make_async_remote_copy(
            parts.at[
                phase, pl.ds(pl.multiple_of(t * tile + target * both, 16), both)
            ],
            plane_in.at[source, phase, pl.ds(t * both, both)],
            plane_send.at[index + target],
            plane_recv.at[index + source],
            **to(z * PLANE + 2 * target + core),
        )

    for t in range(layers):
        block = rows_of_tile(t)
        swap_x[t].wait_recv()
        summed = (
            total[block, :] + transposed_dot(mate_x[:, block], mate_g[...])
        ).astype(jnp.bfloat16)
        for head in range(heads):
            parts[head, block, :] = summed[:, head * head_size : (head + 1) * head_size]
        for step in range(1, spots):
            plane_copy(0, t, step, spot).start()
    for phase in range(1, heads):
        for t in range(layers):
            for step in range(1, spots):
                plane_copy(phase, t, step, spot).start()

    def column_copy(phase, t, side, source):
        index = (phase * layers + t) * 2 + side
        return pltpu.make_async_remote_copy(
            column_part.at[phase, pl.ds(t * both + side * rows, rows)],
            column_in.at[source, phase],
            column_send.at[index],
            column_recv.at[phase * depth + source],
            **to((core * layers + t) * PLANE + 2 * spot + side),
        )

    def is_me(t, side):
        return (core * layers + t) * PLANE + 2 * spot + side == me

    def plane_sum(phase, t):
        for step in range(1, spots):
            plane_copy(phase, t, step, lax.rem(spot + step, spots)).wait_recv()
        value = parts[
            phase, pl.ds(pl.multiple_of(t * tile + spot * both, 16), both), :
        ].astype(jnp.float32)
        for step in range(1, spots):
            value = value + plane_in[
                lax.rem(spot + step, spots), phase, t * both : (t + 1) * both, :
            ].astype(jnp.float32)
        column_part[phase, t * both : (t + 1) * both, :] = value.astype(jnp.bfloat16)
        for side in range(2):
            @pl.when(jnp.logical_not(is_me(t, side)))
            def _():
                column_copy(phase, t, side, z).start()

            @pl.when(is_me(t, side))
            def _():
                column_in[z, phase] = column_part[
                    phase, t * both + side * rows : t * both + (side + 1) * rows, :
                ]

    def line_copy(phase, step, source):
        target = layer(step)
        return pltpu.make_async_remote_copy(
            blocks.at[z, phase],
            blocks.at[source, phase],
            line_send.at[phase * depth + target],
            line_recv.at[phase * depth + source],
            **to(target * PLANE + q),
        )

    def rows_of(owner):
        return pl.ds(pl.multiple_of(owner * rows, 16), rows)

    def row_copy(source, target):
        return pltpu.make_async_remote_copy(
            blocks.at[source, lax.rem(target, heads)],
            tp_out.at[0, rows_of(source * PLANE + q)],
            row_send.at[source * PLANE + target],
            row_recv.at[source * PLANE + q],
            **to(z * PLANE + target),
        )

    def spread(phase, source):
        for target in range(phase, PLANE, heads):
            @pl.when(target != q)
            def _():
                row_copy(source, target).start()

            @pl.when(target == q)
            def _():
                tp_out[0, rows_of(source * PLANE + q), :] = blocks[source, phase]

    def update(phase):
        for source in range(depth):
            @pl.when(source * PLANE + 2 * spot + worker != me)
            def _():
                column_copy(phase, 0, 0, source).wait_recv()
        gradient = column_in[0, phase].astype(jnp.float32)
        for source in range(1, depth):
            gradient = gradient + column_in[source, phase].astype(jnp.float32)
        m_new, v_new, w_new = adam_update(
            gradient, m_ref[:, phase, :], v_ref[:, phase, :], w_ref[:, phase, :]
        )
        blocks[z, phase] = w_new.astype(jnp.bfloat16)
        for step in range(depth - 1, 0, -1):
            line_copy(phase, step, z).start()
        spread(phase, z)
        m_out[:, phase, :] = m_new
        v_out[:, phase, :] = v_new
        w_out[:, phase, :] = w_new

    def forward(phase):
        for step in range(1, depth):
            source = layer(step)
            line_copy(phase, step, source).wait_recv()
            spread(phase, source)

    pieces = [(phase, t) for phase in range(heads) for t in range(layers)]
    for phase in range(heads + 3):
        if phase < heads:
            for t in range(layers):
                plane_sum(phase, t)
        if phase == 1:
            for load in loads[2:]:
                load.wait()
        if 0 <= phase - 1 < heads:
            update(phase - 1)
        if 0 <= phase - 3 < heads:
            forward(phase - 3)
    swap_g.wait_send()
    for swap in swap_x:
        swap.wait_send()
    for phase, t in pieces:
        for step in range(1, spots):
            plane_copy(phase, t, step, spot).wait_send()
        for side in range(2):
            @pl.when(jnp.logical_not(is_me(t, side)))
            def _():
                column_copy(phase, t, side, z).wait_send()
    for phase in range(heads):
        for step in range(1, depth):
            line_copy(phase, step, z).wait_send()
    for source in range(depth):
        for step in range(1, PLANE):
            other = lax.rem(q + step, PLANE)
            row_copy(source, other).wait_send()
            pltpu.make_async_remote_copy(
                blocks.at[0, 0], tp_out.at[0, rows_of(source * PLANE + other)],
                row_send.at[0], row_recv.at[source * PLANE + other], **to(mate),
            ).wait_recv()


def finish_kernel(*refs):
    count = (len(refs) - 1) // 2
    copies = [
        pltpu.make_async_copy(refs[i], refs[count + i], refs[-1].at[i])
        for i in range(count)
    ]
    for copy in copies:
        copy.start()
    for copy in copies:
        copy.wait()


def fused(n, inputs, value_cotangent, master, first_moment, second_moment):
    tokens, features = inputs.shape
    width = value_cotangent.shape[1]
    rows, heads, head_size = master.shape
    half = features // 2
    depth = n // PLANE
    layers = depth // 2
    spots = PLANE // 2
    state = jax.ShapeDtypeStruct(master.shape, jnp.float32)
    block = jax.ShapeDtypeStruct((1, features, head_size), jnp.bfloat16)
    results = 12 * master.size + 2 * block.size + SPARE_BYTES
    vmem = pl.BlockSpec(memory_space=pltpu.VMEM)
    narrow = jnp.bfloat16
    held = pl.pallas_call(
        functools.partial(step_kernel, n),
        out_shape=tuple(pltpu.VMEM(a.shape, a.dtype) for a in (state, state, state, block)),
        in_specs=[pl.BlockSpec(memory_space=pltpu.HBM)] * 5,
        out_specs=[vmem] * 4,
        scratch_shapes=[
            pltpu.VMEM((tokens, features), narrow),
            pltpu.VMEM((tokens, width), narrow),
            pltpu.VMEM(master.shape, jnp.float32),
            pltpu.VMEM(master.shape, jnp.float32),
            pltpu.VMEM(master.shape, jnp.float32),
            pltpu.VMEM((tokens, half), narrow),
            pltpu.VMEM((tokens, width), narrow),
            pltpu.VMEM((half, width), jnp.float32),
            pltpu.VMEM((heads, half, head_size), narrow),
            pltpu.VMEM((spots, heads, layers * 2 * rows, head_size), narrow),
            pltpu.VMEM((heads, layers * 2 * rows, head_size), narrow),
            pltpu.VMEM((depth, heads, rows, head_size), narrow),
            pltpu.VMEM((depth, heads, rows, head_size), narrow),
            pltpu.SemaphoreType.DMA((5,)),
            pltpu.SemaphoreType.DMA((1 + layers,)),
            pltpu.SemaphoreType.DMA((1 + layers,)),
            pltpu.SemaphoreType.DMA((heads * layers * spots,)),
            pltpu.SemaphoreType.DMA((heads * layers * spots,)),
            pltpu.SemaphoreType.DMA((heads * layers * 2,)),
            pltpu.SemaphoreType.DMA((heads * depth,)),
            pltpu.SemaphoreType.DMA((heads * depth,)),
            pltpu.SemaphoreType.DMA((heads * depth,)),
            pltpu.SemaphoreType.DMA((n,)),
            pltpu.SemaphoreType.DMA((n,)),
        ],
        compiler_params=pltpu.CompilerParams(
            collective_id=0, has_side_effects=True, vmem_limit_bytes=VMEM_BYTES - results
        ),
    )(inputs, value_cotangent, master, first_moment, second_moment)
    return pl.pallas_call(
        finish_kernel,
        out_shape=(state, state, state, block),
        in_specs=[vmem] * 4,
        out_specs=[pl.BlockSpec(memory_space=pltpu.HBM)] * 4,
        scratch_shapes=[pltpu.SemaphoreType.DMA((4,))],
        compiler_params=pltpu.CompilerParams(vmem_limit_bytes=VMEM_BYTES // 2),
    )(*held)


def solution(mesh):
    n = mesh.shape["fsdp"]

    def body(inputs, value_cotangent, master, first_moment, second_moment):
        rows = master.shape[0]
        direct = (
            mesh.shape["dp"] == 1
            and n % (2 * PLANE) == 0
            and inputs.shape[1] % (256 * (n // (2 * PLANE))) == 0
            and rows % 16 == 0
            and PLANE % master.shape[1] == 0
            and master.shape[2] % 128 == 0
        )
        if direct:
            return fused(n, inputs, value_cotangent, master, first_moment, second_moment)
        return shards(inputs, value_cotangent, master, first_moment, second_moment)

    placed = (
        P(("fsdp", "dp"), None),
        P(("fsdp", "dp"), None),
        P("fsdp", None, "dp"),
        P("fsdp", None, "dp"),
        P("fsdp", None, "dp"),
    )
    return jax.shard_map(
        body,
        mesh=mesh,
        in_specs=placed,
        out_specs=(
            P("fsdp", None, "dp"),
            P("fsdp", None, "dp"),
            P("fsdp", None, "dp"),
            P("fsdp", None, "dp"),
        ),
        check_vma=False,
    )
```

profile of v0, /device:TPU:11, one launch (start us, length us, event | category | flops | bytes accessed | tf_op | source)
XLA Modules:
  0.0 38.3 jit_solution(2097392550480713367)
XLA Ops:
  0.6 36.6 %shard_map.84 = (f32[80,4,128]{2,1,0:T(4,128)S(1)}, f32[80,4,128]{2,1,0:T(4,128)S(1)}, f32[80,4,128]{2,1,0:T(4,128)S(1)}, bf16[1,2560,128]{2,1,0:T(8,128)(2,1)S(1)}) custom-call(bf16[256,2560]{1,0:T(8,128)(2,1)} %x_hbm.1, bf16[256,512]{1,0:T(8,128)(2,1)} %g_hbm.1, f32[80,4,128]{2,1,0:T(4,128)} %w_hbm.1, f32[80,4,128]{2,1,0:T(4,128)} %m_hbm.1, ...), custom_call_target="tpu_custom_call" | custom-call | tf_op jit(solution)/shard_map/pallas_call | solution.py:324
  37.3 1.0 %shard_map.85 = (f32[80,4,128]{2,1,0:T(4,128)}, f32[80,4,128]{2,1,0:T(4,128)}, f32[80,4,128]{2,1,0:T(4,128)}, bf16[1,2560,128]{2,1,0:T(8,128)(2,1)}) custom-call(f32[80,4,128]{2,1,0:T(4,128)S(1)} %get-tuple-element.8.refs_0_, f32[80,4,128]{2,1,0:T(4,128)S(1)} %get-tuple-element.9.refs_1_, f32[80,4,128]{2,1,0:T(4,128)S(1)} %get-tuple-element.10.refs_2_, ...), custom_call_target="tpu_custom_call" | custom-call | tf_op jit(solution)/shard_map/pallas_call | solution.py:359
where the time goes:
time: 38.5 us; the launch traced here: 38.3 us
  Pallas kernels  37.7 us (98%)
  between operations  0.64 us (2%)
    pallas_call x1, Pallas kernels, fused(): pl.pallas_call(functools.partial(step_kernel, n), out_shape=tuple((pltpu....  36.6 us
    pallas_call x1, Pallas kernels, fused(): pl.pallas_call(finish_kernel, out_shape=(state, state, state, block), in_...  1.04 us

commit v1 on v0

v1 whole, which is shorter than its diff:
```python
import functools

import jax
import jax.numpy as jnp
from jax import lax
from jax.experimental import pallas as pl
from jax.experimental.pallas import tpu as pltpu
from jax.sharding import PartitionSpec as P

STEP = 8


beta_first = 0.9
beta_second = 0.95
learn_rate = 0.001
weight_decay = 0.1
epsilon = 1e-08


def adam_update(gradient, moment_one, moment_two, weights):
    moment_one_new = beta_first * moment_one + (1.0 - beta_first) * gradient
    moment_two_new = beta_second * moment_two + (1.0 - beta_second) * gradient * gradient
    correct_one = 1.0 - beta_first**STEP
    correct_two = 1.0 - beta_second**STEP
    update = (
        moment_one_new / correct_one / (jnp.sqrt(moment_two_new / correct_two) + epsilon)
        + weight_decay * weights
    )
    return (moment_one_new, moment_two_new, weights - learn_rate * update)


def shards(inputs, value_cotangent, master, first_moment, second_moment):
    _, heads, slice_width = master.shape
    head_size = value_cotangent.shape[1] // heads
    head_parts = []
    for head in range(heads):
        head_cot = value_cotangent[:, head * head_size : (head + 1) * head_size]
        head_term = lax.dot_general(
            inputs, head_cot, (((0,), (0,)), ((), ())), preferred_element_type=jnp.float32
        )
        head_parts.append(
            lax.psum_scatter(
                head_term.astype(jnp.bfloat16), "dp", scatter_dimension=1, tiled=True
            ).astype(jnp.float32)
        )
    column_part = jnp.stack(head_parts, axis=1)
    grad_share = lax.psum_scatter(column_part, "fsdp", scatter_dimension=0, tiled=True)
    moment_one_new, moment_two_new, master_new = adam_update(
        grad_share, first_moment, second_moment, master
    )
    narrow_weight = master_new.astype(jnp.bfloat16)
    gathered = lax.all_gather(narrow_weight, "fsdp", axis=0, tiled=True)
    head_index = lax.axis_index("fsdp") % heads
    picked = lax.dynamic_slice_in_dim(gathered, head_index, 1, 1)
    tp_block = picked.reshape(1, gathered.shape[0], slice_width)
    return (moment_one_new, moment_two_new, master_new, tp_block)


VMEM_BYTES = 67043328
SPARE_BYTES = 64 * 1024
PLANE = 8


def step_kernel(
    n, pieces, x_hbm, g_hbm, w_hbm, m_hbm, v_hbm, m_out, v_out, w_out, tp_out,
    x_ref, g_ref, w_ref, m_ref, v_ref,
    mate_x, mate_g, total, parts, first_in, relay, second_in,
    column_part, column_in, blocks,
    load_sem, mate_send, mate_recv, first_send, first_recv, second_send, second_recv,
    column_send, column_recv, row_send, row_recv, side_send, side_recv,
):
    me = lax.axis_index("fsdp")
    z = me // PLANE
    q = lax.rem(me, PLANE)
    y = q // 4
    x = lax.rem(q // 2, 2)
    core = lax.rem(q, 2)
    mate = me + 1 - 2 * core
    x_mate = me + 2 - 4 * x
    y_mate = me + 4 - 8 * y
    depth = n // PLANE
    layers = depth // 2
    rows, heads, head_size = w_ref.shape
    half = x_ref.shape[1] // 2
    tile = half // layers
    worker = z // layers
    turn = z + worker * (depth - 1 - 2 * z)

    def layer(side, t):
        return t + side * (depth - 1 - 2 * t)

    loads = [
        pltpu.make_async_copy(source, target, load_sem.at[i])
        for i, (source, target) in enumerate(
            ((g_hbm, g_ref), (x_hbm, x_ref), (w_hbm, w_ref), (m_hbm, m_ref), (v_hbm, v_ref))
        )
    ]
    for load in loads:
        load.start()

    def to(device):
        return dict(device_id={"fsdp": device}, device_id_type=pl.DeviceIdType.MESH)

    barrier = pltpu.get_barrier_semaphore()
    for step in range(depth):
        for slot in range(4):
            other = lax.rem(z + step, depth) * PLANE + y * 4 + slot
            if step:
                pl.semaphore_signal(barrier, inc=1, **to(other))
            else:
                @pl.when(other != me)
                def _():
                    pl.semaphore_signal(barrier, inc=1, **to(other))
    pl.semaphore_signal(barrier, inc=1, **to(y_mate))
    with jax.named_scope("loads"):
        loads[0].wait()
        loads[1].wait()
    with jax.named_scope("barrier"):
        pl.semaphore_wait(barrier, 4 * depth)

    def columns(side, t):
        return pl.ds(pl.multiple_of(layer(side, t) * tile, 128), tile)

    def rows_of_tile(t):
        return slice(t * tile, (t + 1) * tile)

    swap_g = pltpu.make_async_remote_copy(
        g_ref, mate_g, mate_send.at[0], mate_recv.at[0], **to(mate)
    )
    swap_x = [
        pltpu.make_async_remote_copy(
            x_ref.at[:, columns(1 - core, t)],
            mate_x.at[:, rows_of_tile(t)],
            mate_send.at[1], mate_recv.at[1 + t], **to(mate)
        )
        for t in range(layers)
    ]
    swap_g.start()
    for swap in swap_x:
        swap.start()

    def transposed_dot(left, right):
        return lax.dot_general(
            left, right, (((0,), (0,)), ((), ())), preferred_element_type=jnp.float32
        )

    for t in range(layers):
        total[rows_of_tile(t), :] = transposed_dot(x_ref[:, columns(core, t)], g_ref[...])
    with jax.named_scope("swapg"):
        swap_g.wait_recv()

    def finish_tile(t):
        with jax.named_scope(f"swapx{t}"):
            swap_x[t].wait_recv()
        summed = (
            total[rows_of_tile(t), :]
            + transposed_dot(mate_x[:, rows_of_tile(t)], mate_g[...])
        ).astype(jnp.bfloat16)
        for head in range(heads):
            parts[t, head] = summed[:, head * head_size : (head + 1) * head_size].reshape(
                2, 2, 2, rows, head_size
            )

    def first_copy(k, head):
        t, _, start, count = pieces[k]
        span = pl.ds(start, count)
        if goes_x_first(head):
            source, target = parts.at[t, head, :, 1 - x, :, span], x_mate
        else:
            source, target = parts.at[t, head, 1 - y, :, :, span], y_mate
        return pltpu.make_async_remote_copy(
            source, first_in.at[t, head, :, :, span],
            first_send, first_recv.at[k * heads + head], **to(target)
        )

    def second_copy(k, head):
        t, _, start, count = pieces[k]
        span = pl.ds(start, count)
        return pltpu.make_async_remote_copy(
            relay.at[t, head, :, span], second_in.at[t, head, :, span],
            second_send, second_recv.at[k * heads + head],
            **to(y_mate if goes_x_first(head) else x_mate)
        )

    def column_copy(k, head, side):
        t, group, start, count = pieces[k]
        span = pl.ds(start, count)
        return pltpu.make_async_remote_copy(
            column_part.at[t, head, side, span],
            column_in.at[head, z, span],
            column_send,
            column_recv.at[k],
            **to(layer(core, t) * PLANE + 2 * (q // 2) + side),
        )

    def first(k):
        for head in pieces[k][1]:
            first_copy(k, head).start()

    def second(k):
        t, group, start, count = pieces[k]
        span = slice(start, start + count)
        for head in group:
            with jax.named_scope(f"first{k}_{head}"):
                first_copy(k, head).wait_recv()
            if goes_x_first(head):
                own, came = parts[t, head, 1 - y, x, :, span], first_in[t, head, 1 - y, :, span]
            else:
                own, came = parts[t, head, y, 1 - x, :, span], first_in[t, head, 1 - x, :, span]
            relay[t, head, :, span] = (
                own.astype(jnp.float32) + came.astype(jnp.float32)
            ).astype(jnp.bfloat16)
            second_copy(k, head).start()

    def column(k):
        t, group, start, count = pieces[k]
        span = slice(start, start + count)
        for head in group:
            with jax.named_scope(f"second{k}_{head}"):
                second_copy(k, head).wait_recv()
            came = first_in[t, head, y if goes_x_first(head) else x, :, span]
            value = (
                parts[t, head, y, x, :, span].astype(jnp.float32)
                + came.astype(jnp.float32)
                + second_in[t, head, :, span].astype(jnp.float32)
            ).astype(jnp.bfloat16)
            column_part[t, head, :, span] = value
            for side in range(2):
                own = jnp.logical_and(layer(core, t) == z, core == side)

                @pl.when(jnp.logical_not(own))
                def _():
                    column_copy(k, head, side).start()

                @pl.when(own)
                def _():
                    column_in[head, z, span] = value[side]

    def target_of(layer_to, head):
        return layer_to * PLANE + y * 4 + head

    def row_copy(k, layer_to, head):
        _, _, start, count = pieces[k]
        span = pl.ds(start, count)
        return pltpu.make_async_remote_copy(
            blocks.at[head, span], tp_out.at[me, span],
            row_send, row_recv.at[2 * k + worker], **to(target_of(layer_to, head))
        )

    def update(k):
        t, group, start, count = pieces[k]
        span = slice(start, start + count)

        @pl.when(turn == t)
        def _():
            with jax.named_scope(f"column{k}"):
                for sources, here in ((depth - 1, worker == core), (depth, worker != core)):
                    @pl.when(here)
                    def _():
                        came = column_in.at[pl.ds(0, len(group)), pl.ds(0, sources), pl.ds(0, count)]
                        pltpu.make_async_copy(came, came, column_recv.at[k]).wait()
            news = []
            for head in group:
                gradient = column_in[head, 0, span].astype(jnp.float32)
                for source in range(1, depth):
                    gradient = gradient + column_in[head, source, span].astype(jnp.float32)
                m_new, v_new, w_new = adam_update(
                    gradient, m_ref[span, head, :], v_ref[span, head, :], w_ref[span, head, :]
                )
                narrow = w_new.astype(jnp.bfloat16)
                blocks[head, span] = narrow
                for layer_to in range(depth):
                    @pl.when(target_of(layer_to, head) != me)
                    def _():
                        row_copy(k, layer_to, head).start()

                @pl.when(target_of(z, head) == me)
                def _():
                    tp_out[me, span] = narrow
                news.append((head, m_new, v_new, w_new))
            for head, m_new, v_new, w_new in news:
                m_out[span, head, :] = m_new
                v_out[span, head, :] = v_new
                w_out[span, head, :] = w_new

    def side_copy(k, layer_from):
        _, _, start, count = pieces[k]
        block = tp_out.at[pl.ds(layer_from * PLANE + y * 4, 4), pl.ds(start, count)]
        return pltpu.make_async_remote_copy(block, block, side_send, side_recv, **to(y_mate))

    def forward(k):
        t, group, start, count = pieces[k]

        @pl.when(functools.reduce(jnp.logical_or, [lax.rem(q, 4) == head for head in group]))
        def _():
            for group_worker in range(2):
                layer_from = layer(group_worker, t)
                with jax.named_scope(f"row{k}_{group_worker}"):
                    for slabs, here in ((3, layer_from == z), (4, layer_from != z)):
                        @pl.when(here)
                        def _():
                            came = tp_out.at[pl.ds(0, slabs), pl.ds(0, count)]
                            pltpu.make_async_copy(
                                came, came, row_recv.at[2 * k + group_worker]
                            ).wait()
                side_copy(k, layer_from).start()

    per_tile = len(pieces) // layers
    finish_tile(0)
    issued = 0
    for t in range(layers):
        if t:
            finish_tile(t)
        while issued < min(AHEAD, per_tile * (t + 1)):
            first(issued)
            issued += 1
    for load in loads[2:]:
        load.wait()
    for action, k in schedule(len(pieces)):
        if action == "second":
            second(k)
            if issued < len(pieces):
                first(issued)
                issued += 1
        elif action == "column":
            column(k)
        elif action == "update":
            update(k)
        else:
            forward(k)

    with jax.named_scope("sends"):
        swap_g.wait_send()
        pltpu.make_async_copy(mate_x, mate_x, mate_send.at[1]).wait()
        pltpu.make_async_copy(first_in, first_in, first_send).wait()
        pltpu.make_async_copy(relay, relay, second_send).wait()
        sent = column_part.at[0]
        for _ in range(layers - 1):
            pltpu.make_async_copy(sent, sent, column_send).wait()
        for sides, here in ((1, worker == core), (2, worker != core)):
            @pl.when(here)
            def _():
                last = column_part.at[0, :, pl.ds(0, sides)]
                pltpu.make_async_copy(last, last, column_send).wait()
        slabs = tp_out.at[pl.ds(0, depth * heads - 1)]
        pltpu.make_async_copy(slabs, slabs, row_send).wait()
        slabs = tp_out.at[pl.ds(0, depth * 4)]
        pltpu.make_async_copy(slabs, slabs, side_send).wait()
    with jax.named_scope("last"):
        pltpu.make_async_copy(slabs, slabs, side_recv).wait()


AHEAD = 2
X_FIRST = 2


def goes_x_first(head):
    return head < X_FIRST


def row_pieces(layers, heads, rows):
    return tuple(
        (t, (p, p + 2), 0, rows) for t in range(layers) for p in range(heads // 2)
    )


def schedule(count):
    order = [("second", 0)]
    for k in range(count + 3):
        for action, at in (
            ("second", k + 1), ("column", k), ("forward", k - 3), ("update", k - 1)
        ):
            if 0 <= at < count:
                order.append((action, at))
    return order


def finish_kernel(*refs):
    count = (len(refs) - 1) // 2
    copies = [
        pltpu.make_async_copy(refs[i], refs[count + i], refs[-1].at[i])
        for i in range(count)
    ]
    for copy in copies:
        copy.start()
    for copy in copies:
        copy.wait()


def fused(n, inputs, value_cotangent, master, first_moment, second_moment):
    tokens, features = inputs.shape
    width = value_cotangent.shape[1]
    rows, heads, head_size = master.shape
    half = features // 2
    depth = n // PLANE
    layers = depth // 2
    pieces = row_pieces(layers, heads, rows)
    state = jax.ShapeDtypeStruct(master.shape, jnp.float32)
    slabs = jax.ShapeDtypeStruct((n, rows, head_size), jnp.bfloat16)
    block = jax.ShapeDtypeStruct((1, features, head_size), jnp.bfloat16)
    results = 12 * master.size + 2 * block.size + SPARE_BYTES
    vmem = pl.BlockSpec(memory_space=pltpu.VMEM)
    narrow = jnp.bfloat16
    dma = pltpu.SemaphoreType.DMA
    held = pl.pallas_call(
        functools.partial(step_kernel, n, pieces),
        out_shape=tuple(pltpu.VMEM(a.shape, a.dtype) for a in (state, state, state, slabs)),
        in_specs=[pl.BlockSpec(memory_space=pltpu.HBM)] * 5,
        out_specs=[vmem] * 4,
        scratch_shapes=[
            pltpu.VMEM((tokens, features), narrow),
            pltpu.VMEM((tokens, width), narrow),
            pltpu.VMEM(master.shape, jnp.float32),
            pltpu.VMEM(master.shape, jnp.float32),
            pltpu.VMEM(master.shape, jnp.float32),
            pltpu.VMEM((tokens, half), narrow),
            pltpu.VMEM((tokens, width), narrow),
            pltpu.VMEM((half, width), jnp.float32),
            pltpu.VMEM((layers, heads, 2, 2, 2, rows, head_size), narrow),
            pltpu.VMEM((layers, heads, 2, 2, rows, head_size), narrow),
            pltpu.VMEM((layers, heads, 2, rows, head_size), narrow),
            pltpu.VMEM((layers, heads, 2, rows, head_size), narrow),
            pltpu.VMEM((layers, heads, 2, rows, head_size), narrow),
            pltpu.VMEM((heads, depth, rows, head_size), narrow),
            pltpu.VMEM((heads, rows, head_size), narrow),
            dma((5,)),
            dma((2,)),
            dma((1 + layers,)),
            dma,
            dma((len(pieces) * heads,)),
            dma,
            dma((len(pieces) * heads,)),
            dma,
            dma((len(pieces),)),
            dma,
            dma((2 * len(pieces),)),
            dma,
            dma,
        ],
        compiler_params=pltpu.CompilerParams(
            collective_id=0, has_side_effects=True, vmem_limit_bytes=VMEM_BYTES - results
        ),
    )(inputs, value_cotangent, master, first_moment, second_moment)
    held = held[:3] + (held[3].reshape(block.shape),)
    return pl.pallas_call(
        finish_kernel,
        out_shape=(state, state, state, block),
        in_specs=[vmem] * 4,
        out_specs=[pl.BlockSpec(memory_space=pltpu.HBM)] * 4,
        scratch_shapes=[dma((4,))],
        compiler_params=pltpu.CompilerParams(vmem_limit_bytes=VMEM_BYTES // 2),
    )(*held)


def solution(mesh):
    n = mesh.shape["fsdp"]

    def body(inputs, value_cotangent, master, first_moment, second_moment):
        rows = master.shape[0]
        direct = (
            mesh.shape["dp"] == 1
            and n % (2 * PLANE) == 0
            and inputs.shape[1] % (256 * (n // (2 * PLANE))) == 0
            and rows % 16 == 0
            and master.shape[1] * 2 == PLANE
            and master.shape[2] % 128 == 0
        )
        if direct:
            return fused(n, inputs, value_cotangent, master, first_moment, second_moment)
        return shards(inputs, value_cotangent, master, first_moment, second_moment)

    placed = (
        P(("fsdp", "dp"), None),
        P(("fsdp", "dp"), None),
        P("fsdp", None, "dp"),
        P("fsdp", None, "dp"),
        P("fsdp", None, "dp"),
    )
    return jax.shard_map(
        body,
        mesh=mesh,
        in_specs=placed,
        out_specs=(
            P("fsdp", None, "dp"),
            P("fsdp", None, "dp"),
            P("fsdp", None, "dp"),
            P("fsdp", None, "dp"),
        ),
        check_vma=False,
    )
```

time: 38.5 us -> 40.2 us (1.044)
  the two profiles are of different devices: /device:TPU:11 before, /device:TPU:1 now
where the time goes in v1:
time: 40.2 us; the launch traced here: 40.1 us
  Pallas kernels  39.4 us (98%)
  between operations  0.64 us (2%)
    pallas_call x1, Pallas kernels, fused(): pl.pallas_call(functools.partial(step_kernel, n, pieces), out_shape=tuple...  38.4 us
    pallas_call x1, Pallas kernels, fused(): pl.pallas_call(finish_kernel, out_shape=(state, state, state, block), in_...  1.04 us

profile of v1, /device:TPU:1, one launch (start us, length us, event | category | flops | bytes accessed | tf_op | source)
XLA Modules:
  0.0 40.1 jit_solution(10699978912683830939)
XLA Ops:
  0.6 38.4 %shard_map.84 = (f32[80,4,128]{2,1,0:T(4,128)S(1)}, f32[80,4,128]{2,1,0:T(4,128)S(1)}, f32[80,4,128]{2,1,0:T(4,128)S(1)}, bf16[32,80,128]{2,1,0:T(8,128)(2,1)S(1)}) custom-call(bf16[256,2560]{1,0:T(8,128)(2,1)} %x_hbm.1, bf16[256,512]{1,0:T(8,128)(2,1)} %g_hbm.1, f32[80,4,128]{2,1,0:T(4,128)} %w_hbm.1, f32[80,4,128]{2,1,0:T(4,128)} %m_hbm.1, f32[80,4,128]{2,1,0:T(4,128)} %v_hbm.1), custom_call_target="tpu_custom_call" | custom-call | tf_op jit(solution)/shard_map/pallas_call | solution.py:405
  39.0 1.0 %shard_map.85 = (f32[80,4,128]{2,1,0:T(4,128)}, f32[80,4,128]{2,1,0:T(4,128)}, f32[80,4,128]{2,1,0:T(4,128)}, bf16[1,2560,128]{2,1,0:T(8,128)(2,1)}) custom-call(f32[80,4,128]{2,1,0:T(4,128)S(1)} %get-tuple-element.8.refs_0_, f32[80,4,128]{2,1,0:T(4,128)S(1)} %get-tuple-element.9.refs_1_, f32[80,4,128]{2,1,0:T(4,128)S(1)} %get-tuple-element.10.refs_2_, ...), custom_call_target="tpu_custom_call" | custom-call | tf_op jit(solution)/shard_map/pallas_call | solution.py:445

commit v2 on v1

v2 whole, which is shorter than its diff:
```python
import functools

import jax
import jax.numpy as jnp
from jax import lax
from jax.experimental import pallas as pl
from jax.experimental.pallas import tpu as pltpu
from jax.sharding import PartitionSpec as P

STEP = 8


beta_first = 0.9
beta_second = 0.95
learn_rate = 0.001
weight_decay = 0.1
epsilon = 1e-08


def adam_update(gradient, moment_one, moment_two, weights):
    moment_one_new = beta_first * moment_one + (1.0 - beta_first) * gradient
    moment_two_new = beta_second * moment_two + (1.0 - beta_second) * gradient * gradient
    correct_one = 1.0 - beta_first**STEP
    correct_two = 1.0 - beta_second**STEP
    update = (
        moment_one_new / correct_one / (jnp.sqrt(moment_two_new / correct_two) + epsilon)
        + weight_decay * weights
    )
    return (moment_one_new, moment_two_new, weights - learn_rate * update)


def shards(inputs, value_cotangent, master, first_moment, second_moment):
    _, heads, slice_width = master.shape
    head_size = value_cotangent.shape[1] // heads
    head_parts = []
    for head in range(heads):
        head_cot = value_cotangent[:, head * head_size : (head + 1) * head_size]
        head_term = lax.dot_general(
            inputs, head_cot, (((0,), (0,)), ((), ())), preferred_element_type=jnp.float32
        )
        head_parts.append(
            lax.psum_scatter(
                head_term.astype(jnp.bfloat16), "dp", scatter_dimension=1, tiled=True
            ).astype(jnp.float32)
        )
    column_part = jnp.stack(head_parts, axis=1)
    grad_share = lax.psum_scatter(column_part, "fsdp", scatter_dimension=0, tiled=True)
    moment_one_new, moment_two_new, master_new = adam_update(
        grad_share, first_moment, second_moment, master
    )
    narrow_weight = master_new.astype(jnp.bfloat16)
    gathered = lax.all_gather(narrow_weight, "fsdp", axis=0, tiled=True)
    head_index = lax.axis_index("fsdp") % heads
    picked = lax.dynamic_slice_in_dim(gathered, head_index, 1, 1)
    tp_block = picked.reshape(1, gathered.shape[0], slice_width)
    return (moment_one_new, moment_two_new, master_new, tp_block)


VMEM_BYTES = 67043328
SPARE_BYTES = 64 * 1024
PLANE = 8


def step_kernel(
    n, pieces, x_hbm, g_hbm, w_hbm, m_hbm, v_hbm, m_out, v_out, w_out, tp_out,
    x_ref, g_ref, w_ref, m_ref, v_ref,
    total, mate_part, mate_in, parts, first_in, relay, second_in,
    column_part, column_in, blocks,
    load_sem, mate_send, mate_recv, plane_send, first_recv, second_recv,
    column_send, column_recv, row_send, row_recv, far_send, side_send, side_recv,
    up_sem, down_sem,
):
    me = lax.axis_index("fsdp")
    z = me // PLANE
    q = lax.rem(me, PLANE)
    y = q // 4
    x = lax.rem(q // 2, 2)
    core = lax.rem(q, 2)
    mate = me + 1 - 2 * core
    x_mate = me + 2 - 4 * x
    y_mate = me + 4 - 8 * y
    xy_mate = x_mate + 4 - 8 * y
    depth = n // PLANE
    layers = depth // 2
    rows, heads, head_size = w_ref.shape
    half = x_ref.shape[1] // 2
    tile = half // layers
    worker = z // layers

    def mirrored(place):
        return place + worker * (depth - 1 - 2 * place)

    inward = mirrored(z)

    def layer(side, t):
        return t + side * (depth - 1 - 2 * t)

    loads = [
        pltpu.make_async_copy(source, target, load_sem.at[i])
        for i, (source, target) in enumerate(
            ((g_hbm, g_ref), (x_hbm, x_ref), (w_hbm, w_ref), (m_hbm, m_ref), (v_hbm, v_ref))
        )
    ]
    for load in loads:
        load.start()

    def to(device):
        return dict(device_id={"fsdp": device}, device_id_type=pl.DeviceIdType.MESH)

    barrier = pltpu.get_barrier_semaphore()
    for slot in range(4):
        @pl.when(lax.rem(q, 4) != slot)
        def _():
            pl.semaphore_signal(barrier, inc=1, **to(z * PLANE + y * 4 + slot))
    pl.semaphore_signal(barrier, inc=1, **to(y_mate))
    has_lower, has_upper = z > 0, z < depth - 1

    @pl.when(has_lower)
    def _():
        pl.semaphore_signal(barrier, inc=1, **to(me - PLANE))

    @pl.when(has_upper)
    def _():
        pl.semaphore_signal(barrier, inc=1, **to(me + PLANE))

    def point(p):
        for rank, behind, ahead, semaphore, step in (
            (z, has_lower, has_upper, up_sem, PLANE),
            (depth - 1 - z, has_upper, has_lower, down_sem, -PLANE),
        ):
            @pl.when(rank == p if p < POINTS else rank >= p)
            def _():
                @pl.when(behind)
                def _():
                    pl.semaphore_wait(semaphore, 1)

                @pl.when(ahead)
                def _():
                    pl.semaphore_signal(semaphore, inc=1, **to(me + step))

    with jax.named_scope("loads"):
        loads[0].wait()
        loads[1].wait()

    def dot_tile(side, t):
        columns = pl.ds(pl.multiple_of(layer(side, t) * tile, 128), tile)
        return lax.dot_general(
            x_ref[:, columns], g_ref[...], (((0,), (0,)), ((), ())),
            preferred_element_type=jnp.float32,
        ).reshape(2, 2, 2, rows, heads * head_size)

    def span_of(k):
        start, count = pieces[k][:2]
        return pl.ds(start, count)

    def slice_of(k):
        start, count = pieces[k][:2]
        return slice(start, start + count)

    def mate_copy(k, t):
        span = span_of(k)
        return pltpu.make_async_remote_copy(
            mate_part.at[t, :, :, :, span], mate_in.at[t, :, :, :, span],
            mate_send, mate_recv.at[k * layers + t], **to(mate)
        )

    def first_copies(k, t):
        span = span_of(k)
        arrived = first_recv.at[k * layers + t]
        if not pieces[k][2]:
            moves = (
                (parts.at[t, y, 1 - x, :, span], first_in.at[t, 0, :, span], x_mate),
                (parts.at[t, 1 - y, x, :, span], first_in.at[t, 1, :, span], y_mate),
                (parts.at[t, 1 - y, 1 - x, :, span], second_in.at[t, :, span], xy_mate),
            )
        elif t % 2 == 0:
            moves = ((parts.at[t, :, 1 - x, :, span], first_in.at[t, :, :, span], x_mate),)
        else:
            moves = ((parts.at[t, 1 - y, :, :, span], first_in.at[t, :, :, span], y_mate),)
        return [
            pltpu.make_async_remote_copy(source, target, plane_send, arrived, **to(device))
            for source, target, device in moves
        ]

    def second_copy(k, t):
        span = span_of(k)
        return pltpu.make_async_remote_copy(
            relay.at[t, :, span], second_in.at[t, :, span],
            plane_send, second_recv.at[k * layers + t],
            **to(y_mate if t % 2 == 0 else x_mate)
        )

    def column_copy(k, t, side):
        span = span_of(k)
        return pltpu.make_async_remote_copy(
            column_part.at[t, side, span], column_in.at[z, span],
            column_send, column_recv.at[k],
            **to(layer(core, t) * PLANE + 2 * (q // 2) + side),
        )

    def drain(block, semaphore):
        pltpu.make_async_copy(block, block, semaphore).wait()

    def join(k, t):
        span = slice_of(k)
        with jax.named_scope(f"mate{k}_{t}"):
            mate_copy(k, t).wait_recv()
        parts[t, :, :, :, span] = (
            total[t, :, :, :, span] + mate_in[t, :, :, :, span].astype(jnp.float32)
        ).astype(jnp.bfloat16)
        for copy in first_copies(k, t):
            copy.start()

    def second(k):
        span = slice_of(k)
        if not pieces[k][2]:
            return
        for t in range(layers):
            with jax.named_scope(f"first{k}_{t}"):
                drain(first_in.at[t, :, :, span_of(k)], first_recv.at[k * layers + t])
            if t % 2 == 0:
                own, came = parts[t, 1 - y, x, :, span], first_in[t, 1 - y, :, span]
            else:
                own, came = parts[t, y, 1 - x, :, span], first_in[t, 1 - x, :, span]
            relay[t, :, span] = (
                own.astype(jnp.float32) + came.astype(jnp.float32)
            ).astype(jnp.bfloat16)
            second_copy(k, t).start()

    def column(k):
        span = slice_of(k)
        for t in range(layers):
            if pieces[k][2]:
                with jax.named_scope(f"second{k}_{t}"):
                    second_copy(k, t).wait_recv()
                came = first_in[t, y if t % 2 == 0 else x, :, span].astype(jnp.float32)
            else:
                with jax.named_scope(f"plane{k}_{t}"):
                    for _ in range(3):
                        drain(relay.at[t, :, span_of(k)], first_recv.at[k * layers + t])
                came = first_in[t, 0, :, span].astype(jnp.float32) + first_in[
                    t, 1, :, span
                ].astype(jnp.float32)
            value = (
                parts[t, y, x, :, span].astype(jnp.float32)
                + came
                + second_in[t, :, span].astype(jnp.float32)
            ).astype(jnp.bfloat16)
            column_part[t, :, span] = value
            for side in range(2):
                own = jnp.logical_and(layer(core, t) == z, core == side)

                @pl.when(jnp.logical_not(own))
                def _():
                    column_copy(k, t, side).start()

                @pl.when(own)
                def _():
                    column_in[z, span] = value[side]

    def target_of(layer_to, head):
        return layer_to * PLANE + y * 4 + head

    def reach(k):
        return layers + 1 if pieces[k][3] else depth

    def row_copy(k, layer_to, head):
        span = span_of(k)
        return pltpu.make_async_remote_copy(
            blocks.at[head, span], tp_out.at[me, span],
            row_send, row_recv.at[k * depth + z], **to(target_of(layer_to, head))
        )

    def update(k):
        span = slice_of(k)
        with jax.named_scope(f"column{k}"):
            for sources, here in ((depth - 1, worker == core), (depth, worker != core)):
                @pl.when(here)
                def _():
                    drain(column_in.at[pl.ds(0, sources), span_of(k)], column_recv.at[k])
        gradients = column_in[0, span].astype(jnp.float32)
        for source in range(1, depth):
            gradients = gradients + column_in[source, span].astype(jnp.float32)
        news = []
        for head in range(heads):
            m_new, v_new, w_new = adam_update(
                gradients[:, head * head_size : (head + 1) * head_size],
                m_ref[span, head, :], v_ref[span, head, :], w_ref[span, head, :],
            )
            narrow = w_new.astype(jnp.bfloat16)
            blocks[head, span] = narrow
            news.append((m_new, v_new, w_new))
        for place in reversed(range(reach(k))):
            for head in range(heads):
                target = target_of(mirrored(place), head)

                @pl.when(target != me)
                def _():
                    row_copy(k, mirrored(place), head).start()

        tp_out[me, span] = blocks[lax.rem(q, 4), span]
        for head, (m_new, v_new, w_new) in enumerate(news):
            m_out[span, head, :] = m_new
            v_out[span, head, :] = v_new
            w_out[span, head, :] = w_new

    def group_copy(k, layer_from, device, send, recv):
        block = tp_out.at[pl.ds(layer_from * PLANE + y * 4, 4), span_of(k)]
        return pltpu.make_async_remote_copy(block, block, send, recv, **to(device))

    def forward(k, places, relayed):
        for place in places:
            layer_from = mirrored(place)
            arrived = row_recv.at[k * depth + layer_from]
            with jax.named_scope(f"row{k}_{place}"):
                if place < layers:
                    for slabs, here in ((3, inward == place), (4, inward != place)):
                        @pl.when(here)
                        def _():
                            drain(tp_out.at[pl.ds(0, slabs), span_of(k)], arrived)
                else:
                    drain(tp_out.at[pl.ds(0, 4), span_of(k)], arrived)
            if relayed:
                for other in range(layers - 1):
                    group_copy(
                        k, layer_from, mirrored(other) * PLANE + q, far_send, arrived
                    ).start()
            group_copy(k, layer_from, y_mate, side_send, side_recv).start()

    def near(k):
        forward(k, range(layers), False)

    def gate(k):
        @pl.when(inward == layers - 1)
        def _():
            forward(k, range(layers, depth), pieces[k][3])

    def end(k):
        @pl.when(inward != layers - 1)
        def _():
            forward(k, range(layers, depth), False)

    for t in range(layers):
        mate_part[t] = dot_tile(1 - core, t).astype(jnp.bfloat16)
        if t == 0:
            with jax.named_scope("barrier"):
                pl.semaphore_wait(
                    barrier, 4 + has_lower.astype(jnp.int32) + has_upper.astype(jnp.int32)
                )
            point(0)
        mate_copy(0, t).start()
        total[t] = dot_tile(core, t)
        if t:
            for k in range(1, len(pieces)):
                for other in range(layers):
                    mate_copy(k, other).start()

    for load in loads[2:]:
        load.wait()
    for action, k in ORDER:
        if action == "join":
            for t in range(layers):
                join(k, t)
        elif action == "point":
            with jax.named_scope(f"point{k}"):
                point(k)
        elif action == "second":
            second(k)
        elif action == "column":
            column(k)
        elif action == "update":
            update(k)
        else:
            {"near": near, "gate": gate, "end": end}[action](k)

    with jax.named_scope("sends"):
        drain(mate_part, mate_send)
        for k in range(len(pieces)):
            span = span_of(k)
            if pieces[k][2]:
                drain(first_in.at[:, :, :, span], plane_send)
                drain(relay.at[:, :, span], plane_send)
            else:
                for _ in range(3):
                    drain(relay.at[:, :, span], plane_send)
        for sides, here in ((1, worker == core), (2, worker != core)):
            @pl.when(here)
            def _():
                for t in range(layers):
                    drain(column_part.at[t, pl.ds(0, sides if t == 0 else 2)], column_send)
        for k in range(len(pieces)):
            drain(tp_out.at[pl.ds(0, heads * reach(k) - 1), span_of(k)], row_send)
            if pieces[k][3] and layers > 1:
                @pl.when(inward == layers - 1)
                def _():
                    for _ in range(layers - 1):
                        drain(tp_out.at[pl.ds(0, 4 * layers), span_of(k)], far_send)
        slabs = tp_out.at[pl.ds(0, depth * 4)]
        drain(slabs, side_send)
    with jax.named_scope("last"):
        drain(slabs, side_recv)


POINTS = 3
PARTS = ((16, True, True),) * 5
ORDER = (
    ("join", 0), ("join", 1), ("join", 2), ("point", 1), ("second", 0), ("join", 3),
    ("point", 2), ("second", 1), ("join", 4), ("second", 2), ("point", 3), ("column", 0),
    ("second", 3), ("column", 1), ("second", 4), ("column", 2), ("update", 0), ("column", 3),
    ("column", 4), ("update", 1), ("near", 0), ("gate", 0), ("update", 2), ("near", 1),
    ("update", 3), ("gate", 1), ("end", 0), ("update", 4), ("near", 2), ("gate", 2),
    ("near", 3), ("gate", 3), ("end", 1), ("end", 2), ("near", 4), ("gate", 4), ("end", 3),
    ("end", 4),
)


def row_pieces(rows):
    pieces, start = [], 0
    for i, (share, twice, deputed) in enumerate(PARTS):
        count = rows - start if i + 1 == len(PARTS) else share
        pieces.append((start, count, twice, deputed))
        start += count
    return tuple(pieces)


def finish_kernel(*refs):
    count = (len(refs) - 1) // 2
    copies = [
        pltpu.make_async_copy(refs[i], refs[count + i], refs[-1].at[i])
        for i in range(count)
    ]
    for copy in copies:
        copy.start()
    for copy in copies:
        copy.wait()


def fused(n, inputs, value_cotangent, master, first_moment, second_moment):
    tokens, features = inputs.shape
    width = value_cotangent.shape[1]
    rows, heads, head_size = master.shape
    depth = n // PLANE
    layers = depth // 2
    pieces = row_pieces(rows)
    state = jax.ShapeDtypeStruct(master.shape, jnp.float32)
    slabs = jax.ShapeDtypeStruct((n, rows, head_size), jnp.bfloat16)
    block = jax.ShapeDtypeStruct((1, features, head_size), jnp.bfloat16)
    results = 12 * master.size + 2 * block.size + SPARE_BYTES
    vmem = pl.BlockSpec(memory_space=pltpu.VMEM)
    narrow = jnp.bfloat16
    dma = pltpu.SemaphoreType.DMA
    held = pl.pallas_call(
        functools.partial(step_kernel, n, pieces),
        out_shape=tuple(pltpu.VMEM(a.shape, a.dtype) for a in (state, state, state, slabs)),
        in_specs=[pl.BlockSpec(memory_space=pltpu.HBM)] * 5,
        out_specs=[vmem] * 4,
        scratch_shapes=[
            pltpu.VMEM((tokens, features), narrow),
            pltpu.VMEM((tokens, width), narrow),
            pltpu.VMEM(master.shape, jnp.float32),
            pltpu.VMEM(master.shape, jnp.float32),
            pltpu.VMEM(master.shape, jnp.float32),
            pltpu.VMEM((layers, 2, 2, 2, rows, width), jnp.float32),
            pltpu.VMEM((layers, 2, 2, 2, rows, width), narrow),
            pltpu.VMEM((layers, 2, 2, 2, rows, width), narrow),
            pltpu.VMEM((layers, 2, 2, 2, rows, width), narrow),
            pltpu.VMEM((layers, 2, 2, rows, width), narrow),
            pltpu.VMEM((layers, 2, rows, width), narrow),
            pltpu.VMEM((layers, 2, rows, width), narrow),
            pltpu.VMEM((layers, 2, rows, width), narrow),
            pltpu.VMEM((depth, rows, width), narrow),
            pltpu.VMEM((heads, rows, head_size), narrow),
            dma((5,)),
            dma,
            dma((layers * len(pieces),)),
            dma,
            dma((layers * len(pieces),)),
            dma((layers * len(pieces),)),
            dma,
            dma((len(pieces),)),
            dma,
            dma((depth * len(pieces),)),
            dma,
            dma,
            dma,
            pltpu.SemaphoreType.REGULAR,
            pltpu.SemaphoreType.REGULAR,
        ],
        compiler_params=pltpu.CompilerParams(
            collective_id=0, has_side_effects=True, vmem_limit_bytes=VMEM_BYTES - results
        ),
    )(inputs, value_cotangent, master, first_moment, second_moment)
    held = held[:3] + (held[3].reshape(block.shape),)
    return pl.pallas_call(
        finish_kernel,
        out_shape=(state, state, state, block),
        in_specs=[vmem] * 4,
        out_specs=[pl.BlockSpec(memory_space=pltpu.HBM)] * 4,
        scratch_shapes=[dma((4,))],
        compiler_params=pltpu.CompilerParams(vmem_limit_bytes=VMEM_BYTES // 2),
    )(*held)


def solution(mesh):
    n = mesh.shape["fsdp"]

    def body(inputs, value_cotangent, master, first_moment, second_moment):
        rows = master.shape[0]
        direct = (
            mesh.shape["dp"] == 1
            and n % (2 * PLANE) == 0
            and inputs.shape[1] % (256 * (n // (2 * PLANE))) == 0
            and rows % 16 == 0
            and rows > sum(part[0] for part in PARTS[:-1])
            and master.shape[1] * 2 == PLANE
            and master.shape[2] % 128 == 0
        )
        if direct:
            return fused(n, inputs, value_cotangent, master, first_moment, second_moment)
        return shards(inputs, value_cotangent, master, first_moment, second_moment)

    placed = (
        P(("fsdp", "dp"), None),
        P(("fsdp", "dp"), None),
        P("fsdp", None, "dp"),
        P("fsdp", None, "dp"),
        P("fsdp", None, "dp"),
    )
    return jax.shard_map(
        body,
        mesh=mesh,
        in_specs=placed,
        out_specs=(
            P("fsdp", None, "dp"),
            P("fsdp", None, "dp"),
            P("fsdp", None, "dp"),
            P("fsdp", None, "dp"),
        ),
        check_vma=False,
    )
```

time: 40.2 us -> 37.5 us (0.933)
  the two profiles are of different devices: /device:TPU:1 before, /device:TPU:0 now
where the time goes in v2:
time: 37.5 us; the launch traced here: 37.3 us
  Pallas kernels  36.7 us (98%)
  between operations  0.64 us (2%)
    pallas_call x1, Pallas kernels, fused(): pl.pallas_call(functools.partial(step_kernel, n, pieces), out_shape=tuple...  35.6 us
    pallas_call x1, Pallas kernels, fused(): pl.pallas_call(finish_kernel, out_shape=(state, state, state, block), in_...  1.04 us

profile of v2, /device:TPU:0, one launch (start us, length us, event | category | flops | bytes accessed | tf_op | source)
XLA Modules:
  0.0 37.3 jit_solution(12280788626587337786)
XLA Ops:
  0.6 35.6 %shard_map.84 = (f32[80,4,128]{2,1,0:T(4,128)S(1)}, f32[80,4,128]{2,1,0:T(4,128)S(1)}, f32[80,4,128]{2,1,0:T(4,128)S(1)}, bf16[32,80,128]{2,1,0:T(8,128)(2,1)S(1)}) custom-call(bf16[256,2560]{1,0:T(8,128)(2,1)} %x_hbm.1, bf16[256,512]{1,0:T(8,128)(2,1)} %g_hbm.1, f32[80,4,128]{2,1,0:T(4,128)} %w_hbm.1, f32[80,4,128]{2,1,0:T(4,128)} %m_hbm.1, f32[80,4,128]{2,1,0:T(4,128)} %v_hbm.1), custom_call_target="tpu_custom_call" | custom-call | tf_op jit(solution)/shard_map/pallas_call | solution.py:452
  36.3 1.0 %shard_map.85 = (f32[80,4,128]{2,1,0:T(4,128)}, f32[80,4,128]{2,1,0:T(4,128)}, f32[80,4,128]{2,1,0:T(4,128)}, bf16[1,2560,128]{2,1,0:T(8,128)(2,1)}) custom-call(f32[80,4,128]{2,1,0:T(4,128)S(1)} %get-tuple-element.8.refs_0_, f32[80,4,128]{2,1,0:T(4,128)S(1)} %get-tuple-element.9.refs_1_, f32[80,4,128]{2,1,0:T(4,128)S(1)} %get-tuple-element.10.refs_2_, ...), custom_call_target="tpu_custom_call" | custom-call | tf_op jit(solution)/shard_map/pallas_call | solution.py:494

commit v3 on v2

--- a/solution.py
+++ b/solution.py
@@ -65,10 +65,10 @@
     n, pieces, x_hbm, g_hbm, w_hbm, m_hbm, v_hbm, m_out, v_out, w_out, tp_out,
     x_ref, g_ref, w_ref, m_ref, v_ref,
     total, mate_part, mate_in, parts, first_in, relay, second_in,
-    column_part, column_in, blocks,
+    column_part, column_in, line_in, line_sum, plane_part, plane_in, blocks,
     load_sem, mate_send, mate_recv, plane_send, first_recv, second_recv,
     column_send, column_recv, row_send, row_recv, far_send, side_send, side_recv,
-    up_sem, down_sem,
+    line_recv, plane_recv, up_sem, down_sem,
 ):
     me = lax.axis_index("fsdp")
     z = me // PLANE
@@ -167,13 +167,7 @@
     def first_copies(k, t):
         span = span_of(k)
         arrived = first_recv.at[k * layers + t]
-        if not pieces[k][2]:
-            moves = (
-                (parts.at[t, y, 1 - x, :, span], first_in.at[t, 0, :, span], x_mate),
-                (parts.at[t, 1 - y, x, :, span], first_in.at[t, 1, :, span], y_mate),
-                (parts.at[t, 1 - y, 1 - x, :, span], second_in.at[t, :, span], xy_mate),
-            )
-        elif t % 2 == 0:
+        if t % 2 == 0:
             moves = ((parts.at[t, :, 1 - x, :, span], first_in.at[t, :, :, span], x_mate),)
         else:
             moves = ((parts.at[t, 1 - y, :, :, span], first_in.at[t, :, :, span], y_mate),)
@@ -205,16 +199,52 @@
         span = slice_of(k)
         with jax.named_scope(f"mate{k}_{t}"):
             mate_copy(k, t).wait_recv()
-        parts[t, :, :, :, span] = (
+        value = (
             total[t, :, :, :, span] + mate_in[t, :, :, :, span].astype(jnp.float32)
         ).astype(jnp.bfloat16)
-        for copy in first_copies(k, t):
-            copy.start()
+        parts[t, :, :, :, span] = value
+        if pieces[k][2]:
+            for copy in first_copies(k, t):
+                copy.start()
+            return
+        for side in range(2):
+            own = jnp.logical_and(layer(core, t) == z, core == side)
+
+            @pl.when(jnp.logical_not(own))
+            def _():
+                pltpu.make_async_remote_copy(
+                    parts.at[t, :, :, side, span_of(k)], line_in.at[z], plane_send, line_recv,
+                    **to(layer(core, t) * PLANE + 2 * (q // 2) + side)
+                ).start()
+
+            @pl.when(own)
+            def _():
+                line_in[z] = value[:, :, side]
+
+    def across(k):
+        with jax.named_scope(f"line{k}"):
+            for sources, here in ((depth - 1, worker == core), (depth, worker != core)):
+                @pl.when(here)
+                def _():
+                    drain(line_in.at[pl.ds(0, sources)], line_recv)
+        value = line_in[0].astype(jnp.float32)
+        for source in range(1, depth):
+            value = value + line_in[source].astype(jnp.float32)
+        plane_part[...] = value.astype(jnp.bfloat16)
+        for slot, (row, column_at, device) in enumerate(
+            ((y, 1 - x, x_mate), (1 - y, x, y_mate), (1 - y, 1 - x, xy_mate))
+        ):
+            pltpu.make_async_remote_copy(
+                plane_part.at[row, column_at], plane_in.at[slot], plane_send, plane_recv,
+                **to(device)
+            ).start()
+        own = line_in[0, y, x].astype(jnp.float32)
+        for source in range(1, depth):
+            own = own + line_in[source, y, x].astype(jnp.float32)
+        line_sum[...] = own
 
     def second(k):
         span = slice_of(k)
-        if not pieces[k][2]:
-            return
         for t in range(layers):
             with jax.named_scope(f"first{k}_{t}"):
                 drain(first_in.at[t, :, :, span_of(k)], first_recv.at[k * layers + t])
@@ -230,17 +260,9 @@
     def column(k):
         span = slice_of(k)
         for t in range(layers):
-            if pieces[k][2]:
-                with jax.named_scope(f"second{k}_{t}"):
-                    second_copy(k, t).wait_recv()
-                came = first_in[t, y if t % 2 == 0 else x, :, span].astype(jnp.float32)
-            else:
-                with jax.named_scope(f"plane{k}_{t}"):
-                    for _ in range(3):
-                        drain(relay.at[t, :, span_of(k)], first_recv.at[k * layers + t])
-                came = first_in[t, 0, :, span].astype(jnp.float32) + first_in[
-                    t, 1, :, span
-                ].astype(jnp.float32)
+            with jax.named_scope(f"second{k}_{t}"):
+                second_copy(k, t).wait_recv()
+            came = first_in[t, y if t % 2 == 0 else x, :, span].astype(jnp.float32)
             value = (
                 parts[t, y, x, :, span].astype(jnp.float32)
                 + came
@@ -274,13 +296,19 @@
     def update(k):
         span = slice_of(k)
         with jax.named_scope(f"column{k}"):
-            for sources, here in ((depth - 1, worker == core), (depth, worker != core)):
-                @pl.when(here)
-                def _():
-                    drain(column_in.at[pl.ds(0, sources), span_of(k)], column_recv.at[k])
-        gradients = column_in[0, span].astype(jnp.float32)
-        for source in range(1, depth):
-            gradients = gradients + column_in[source, span].astype(jnp.float32)
+            if pieces[k][2]:
+                for sources, here in ((depth - 1, worker == core), (depth, worker != core)):
+                    @pl.when(here)
+                    def _():
+                        drain(column_in.at[pl.ds(0, sources), span_of(k)], column_recv.at[k])
+                gradients = column_in[0, span].astype(jnp.float32)
+                for source in range(1, depth):
+                    gradients = gradients + column_in[source, span].astype(jnp.float32)
+            else:
+                drain(plane_in, plane_recv)
+                gradients = line_sum[...]
+                for source in range(3):
+                    gradients = gradients + plane_in[source].astype(jnp.float32)
         news = []
         for head in range(heads):
             m_new, v_new, w_new = adam_update(
@@ -368,6 +396,8 @@
             second(k)
         elif action == "column":
             column(k)
+        elif action == "across":
+            across(k)
         elif action == "update":
             update(k)
         else:
@@ -381,13 +411,24 @@
                 drain(first_in.at[:, :, :, span], plane_send)
                 drain(relay.at[:, :, span], plane_send)
             else:
-                for _ in range(3):
-                    drain(relay.at[:, :, span], plane_send)
-        for sides, here in ((1, worker == core), (2, worker != core)):
-            @pl.when(here)
-            def _():
-                for t in range(layers):
-                    drain(column_part.at[t, pl.ds(0, sides if t == 0 else 2)], column_send)
+                drain(plane_in, plane_send)
+                for _ in range(layers * 2 - 1):
+                    drain(plane_part, plane_send)
+
+                @pl.when(worker != core)
+                def _():
+                    drain(plane_part, plane_send)
+        for k in range(len(pieces)):
+            if not pieces[k][2]:
+                continue
+            for sides, here in ((1, worker == core), (2, worker != core)):
+                @pl.when(here)
+                def _():
+                    for t in range(layers):
+                        drain(
+                            column_part.at[t, pl.ds(0, sides if t == 0 else 2), span_of(k)],
+                            column_send,
+                        )
         for k in range(len(pieces)):
             drain(tp_out.at[pl.ds(0, heads * reach(k) - 1), span_of(k)], row_send)
             if pieces[k][3] and layers > 1:
@@ -402,15 +443,14 @@
 
 
 POINTS = 3
-PARTS = ((16, True, True),) * 5
+PARTS = ((16, True, True),) * 4 + ((16, False, True),)
 ORDER = (
-    ("join", 0), ("join", 1), ("join", 2), ("point", 1), ("second", 0), ("join", 3),
-    ("point", 2), ("second", 1), ("join", 4), ("second", 2), ("point", 3), ("column", 0),
-    ("second", 3), ("column", 1), ("second", 4), ("column", 2), ("update", 0), ("column", 3),
-    ("column", 4), ("update", 1), ("near", 0), ("gate", 0), ("update", 2), ("near", 1),
-    ("update", 3), ("gate", 1), ("end", 0), ("update", 4), ("near", 2), ("gate", 2),
-    ("near", 3), ("gate", 3), ("end", 1), ("end", 2), ("near", 4), ("gate", 4), ("end", 3),
-    ("end", 4),
+    ("join", 0), ("join", 1), ("join", 2), ("point", 1), ("point", 2), ("point", 3),
+    ("join", 4), ("second", 0), ("join", 3), ("second", 1), ("second", 2), ("column", 0),
+    ("second", 3), ("column", 1), ("column", 2), ("update", 0), ("column", 3), ("across", 4),
+    ("update", 1), ("near", 0), ("update", 4), ("gate", 0), ("update", 2), ("near", 1),
+    ("update", 3), ("gate", 1), ("near", 4), ("gate", 4), ("end", 0), ("near", 2), ("gate", 2),
+    ("near", 3), ("gate", 3), ("end", 1), ("end", 4), ("end", 2), ("end", 3),
 )
 
 
@@ -469,6 +509,10 @@
             pltpu.VMEM((layers, 2, rows, width), narrow),
             pltpu.VMEM((layers, 2, rows, width), narrow),
             pltpu.VMEM((depth, rows, width), narrow),
+            pltpu.VMEM((depth, 2, 2, pieces[-1][1], width), narrow),
+            pltpu.VMEM((pieces[-1][1], width), jnp.float32),
+            pltpu.VMEM((2, 2, pieces[-1][1], width), narrow),
+            pltpu.VMEM((3, pieces[-1][1], width), narrow),
             pltpu.VMEM((heads, rows, head_size), narrow),
             dma((5,)),
             dma,
@@ -480,6 +524,8 @@
             dma((len(pieces),)),
             dma,
             dma((depth * len(pieces),)),
+            dma,
+            dma,
             dma,
             dma,
             dma,

time: 37.5 us -> 35.3 us (0.941)
  Pallas kernels: 36.7 us -> 34.5 us
    pallas_call x1, Pallas kernels: 35.6 us -> 33.4 us  [fused(): pl.pallas_call(functools.partial(step_kernel, n, pieces), out_shape=tuple...]
where the time goes in v3:
time: 35.3 us; the launch traced here: 35.1 us
  Pallas kernels  34.5 us (98%)
  between operations  0.64 us (2%)
    pallas_call x1, Pallas kernels, fused(): pl.pallas_call(functools.partial(step_kernel, n, pieces), out_shape=tuple...  33.4 us
    pallas_call x1, Pallas kernels, fused(): pl.pallas_call(finish_kernel, out_shape=(state, state, state, block), in_...  1.04 us

profile of v3, /device:TPU:0, one launch (start us, length us, event | category | flops | bytes accessed | tf_op | source)
XLA Modules:
  0.0 35.1 jit_solution(3372647556939826438)
XLA Ops:
  0.6 33.4 %shard_map.84 = (f32[80,4,128]{2,1,0:T(4,128)S(1)}, f32[80,4,128]{2,1,0:T(4,128)S(1)}, f32[80,4,128]{2,1,0:T(4,128)S(1)}, bf16[32,80,128]{2,1,0:T(8,128)(2,1)S(1)}) custom-call(bf16[256,2560]{1,0:T(8,128)(2,1)} %x_hbm.1, bf16[256,512]{1,0:T(8,128)(2,1)} %g_hbm.1, f32[80,4,128]{2,1,0:T(4,128)} %w_hbm.1, f32[80,4,128]{2,1,0:T(4,128)} %m_hbm.1, f32[80,4,128]{2,1,0:T(4,128)} %v_hbm.1), custom_call_target="tpu_custom_call" | custom-call | tf_op jit(solution)/shard_map/pallas_call | solution.py:492
  34.1 1.0 %shard_map.85 = (f32[80,4,128]{2,1,0:T(4,128)}, f32[80,4,128]{2,1,0:T(4,128)}, f32[80,4,128]{2,1,0:T(4,128)}, bf16[1,2560,128]{2,1,0:T(8,128)(2,1)}) custom-call(f32[80,4,128]{2,1,0:T(4,128)S(1)} %get-tuple-element.8.refs_0_, f32[80,4,128]{2,1,0:T(4,128)S(1)} %get-tuple-element.9.refs_1_, f32[80,4,128]{2,1,0:T(4,128)S(1)} %get-tuple-element.10.refs_2_, ...), custom_call_target="tpu_custom_call" | custom-call | tf_op jit(solution)/shard_map/pallas_call | solution.py:540

commit v4 on v3

--- a/solution.py
+++ b/solution.py
@@ -95,13 +95,23 @@
     def layer(side, t):
         return t + side * (depth - 1 - 2 * t)
 
-    loads = [
-        pltpu.make_async_copy(source, target, load_sem.at[i])
-        for i, (source, target) in enumerate(
-            ((g_hbm, g_ref), (x_hbm, x_ref), (w_hbm, w_ref), (m_hbm, m_ref), (v_hbm, v_ref))
-        )
+    def columns(side, t):
+        return pl.ds(pl.multiple_of(layer(side, t) * tile, 128), tile)
+
+    tiles = [(side, t) for side in (1 - core, core) for t in range(layers)]
+    load_g = pltpu.make_async_copy(g_hbm, g_ref, load_sem.at[0])
+    load_x = [
+        pltpu.make_async_copy(
+            x_hbm.at[:, columns(*place)], x_ref.at[:, columns(*place)], load_sem.at[4 + i]
+        )
+        for i, place in enumerate(tiles)
     ]
-    for load in loads:
+    load_state = [
+        pltpu.make_async_copy(source, target, load_sem.at[1 + i])
+        for i, (source, target) in enumerate(((w_hbm, w_ref), (m_hbm, m_ref), (v_hbm, v_ref)))
+    ]
+    load_g.start()
+    for load in load_x + load_state:
         load.start()
 
     def to(device):
@@ -138,14 +148,9 @@
                 def _():
                     pl.semaphore_signal(semaphore, inc=1, **to(me + step))
 
-    with jax.named_scope("loads"):
-        loads[0].wait()
-        loads[1].wait()
-
     def dot_tile(side, t):
-        columns = pl.ds(pl.multiple_of(layer(side, t) * tile, 128), tile)
         return lax.dot_general(
-            x_ref[:, columns], g_ref[...], (((0,), (0,)), ((), ())),
+            x_ref[:, columns(side, t)], g_ref[...], (((0,), (0,)), ((), ())),
             preferred_element_type=jnp.float32,
         ).reshape(2, 2, 2, rows, heads * head_size)
 
@@ -326,6 +331,11 @@
                 def _():
                     row_copy(k, mirrored(place), head).start()
 
+        for head in range(heads):
+            pltpu.make_async_remote_copy(
+                blocks.at[head, span_of(k)], tp_out.at[me, span_of(k)], row_send, side_recv,
+                **to(z * PLANE + (1 - y) * 4 + head)
+            ).start()
         tp_out[me, span] = blocks[lax.rem(q, 4), span]
         for head, (m_new, v_new, w_new) in enumerate(news):
             m_out[span, head, :] = m_new
@@ -336,7 +346,7 @@
         block = tp_out.at[pl.ds(layer_from * PLANE + y * 4, 4), span_of(k)]
         return pltpu.make_async_remote_copy(block, block, send, recv, **to(device))
 
-    def forward(k, places, relayed):
+    def forward(k, places, relayed, crossed):
         for place in places:
             layer_from = mirrored(place)
             arrived = row_recv.at[k * depth + layer_from]
@@ -348,27 +358,38 @@
                             drain(tp_out.at[pl.ds(0, slabs), span_of(k)], arrived)
                 else:
                     drain(tp_out.at[pl.ds(0, 4), span_of(k)], arrived)
-            if relayed:
-                for other in range(layers - 1):
-                    group_copy(
-                        k, layer_from, mirrored(other) * PLANE + q, far_send, arrived
-                    ).start()
-            group_copy(k, layer_from, y_mate, side_send, side_recv).start()
+            for other in range(layers - 1 if relayed else 0):
+                there = mirrored(other) * PLANE + q
+                group_copy(k, layer_from, there, far_send, arrived).start()
+                if relayed == 2:
+                    group_copy(k, layer_from, there + y_mate - me, far_send, side_recv).start()
+            if not crossed:
+                continue
+            if place >= layers:
+                group_copy(k, layer_from, y_mate, side_send, side_recv).start()
+            else:
+                @pl.when(inward != place)
+                def _():
+                    group_copy(k, layer_from, y_mate, side_send, side_recv).start()
 
     def near(k):
-        forward(k, range(layers), False)
+        forward(k, range(layers), 0, True)
 
     def gate(k):
         @pl.when(inward == layers - 1)
         def _():
-            forward(k, range(layers, depth), pieces[k][3])
+            forward(k, range(layers, depth), pieces[k][3], True)
 
     def end(k):
         @pl.when(inward != layers - 1)
         def _():
-            forward(k, range(layers, depth), False)
-
+            forward(k, range(layers, depth), 0, pieces[k][3] != 2)
+
+    with jax.named_scope("loads"):
+        load_g.wait()
     for t in range(layers):
+        with jax.named_scope(f"load{t}"):
+            load_x[t].wait()
         mate_part[t] = dot_tile(1 - core, t).astype(jnp.bfloat16)
         if t == 0:
             with jax.named_scope("barrier"):
@@ -377,13 +398,13 @@
                 )
             point(0)
         mate_copy(0, t).start()
+    for k in range(1, len(pieces)):
+        for t in range(layers):
+            mate_copy(k, t).start()
+    for t in range(layers):
+        load_x[layers + t].wait()
         total[t] = dot_tile(core, t)
-        if t:
-            for k in range(1, len(pieces)):
-                for other in range(layers):
-                    mate_copy(k, other).start()
-
-    for load in loads[2:]:
+    for load in load_state:
         load.wait()
     for action, k in ORDER:
         if action == "join":
@@ -430,24 +451,30 @@
                             column_send,
                         )
         for k in range(len(pieces)):
-            drain(tp_out.at[pl.ds(0, heads * reach(k) - 1), span_of(k)], row_send)
+            drain(tp_out.at[pl.ds(0, heads * (reach(k) + 1) - 1), span_of(k)], row_send)
             if pieces[k][3] and layers > 1:
                 @pl.when(inward == layers - 1)
                 def _():
-                    for _ in range(layers - 1):
+                    for _ in range((layers - 1) * pieces[k][3]):
                         drain(tp_out.at[pl.ds(0, 4 * layers), span_of(k)], far_send)
+            for slabs, here in (
+                ((depth - 1) * 4, inward == layers - 1),
+                (((layers if pieces[k][3] == 2 else depth) - 1) * 4, inward != layers - 1),
+            ):
+                @pl.when(here)
+                def _():
+                    drain(tp_out.at[pl.ds(0, slabs), span_of(k)], side_send)
         slabs = tp_out.at[pl.ds(0, depth * 4)]
-        drain(slabs, side_send)
     with jax.named_scope("last"):
         drain(slabs, side_recv)
 
 
 POINTS = 3
-PARTS = ((16, True, True),) * 4 + ((16, False, True),)
+PARTS = ((16, True, 1), (16, True, 1), (16, True, 1), (16, True, 2), (16, False, 1))
 ORDER = (
     ("join", 0), ("join", 1), ("join", 2), ("point", 1), ("point", 2), ("point", 3),
     ("join", 4), ("second", 0), ("join", 3), ("second", 1), ("second", 2), ("column", 0),
-    ("second", 3), ("column", 1), ("column", 2), ("update", 0), ("column", 3), ("across", 4),
+    ("second", 3), ("across", 4), ("column", 1), ("column", 2), ("update", 0), ("column", 3),
     ("update", 1), ("near", 0), ("update", 4), ("gate", 0), ("update", 2), ("near", 1),
     ("update", 3), ("gate", 1), ("near", 4), ("gate", 4), ("end", 0), ("near", 2), ("gate", 2),
     ("near", 3), ("gate", 3), ("end", 1), ("end", 4), ("end", 2), ("end", 3),
@@ -514,7 +541,7 @@
             pltpu.VMEM((2, 2, pieces[-1][1], width), narrow),
             pltpu.VMEM((3, pieces[-1][1], width), narrow),
             pltpu.VMEM((heads, rows, head_size), narrow),
-            dma((5,)),
+            dma((4 + 2 * layers,)),
             dma,
             dma((layers * len(pieces),)),
             dma,

time: 35.3 us -> 34.7 us (0.983)
  Pallas kernels: 34.5 us -> 33.9 us
    pallas_call x1, Pallas kernels: 33.4 us -> 32.9 us  [fused(): pl.pallas_call(functools.partial(step_kernel, n, pieces), out_shape=tuple...]
where the time goes in v4:
time: 34.7 us; the launch traced here: 34.6 us
  Pallas kernels  33.9 us (98%)
  between operations  0.64 us (2%)
    pallas_call x1, Pallas kernels, fused(): pl.pallas_call(functools.partial(step_kernel, n, pieces), out_shape=tuple...  32.9 us
    pallas_call x1, Pallas kernels, fused(): pl.pallas_call(finish_kernel, out_shape=(state, state, state, block), in_...  1.04 us

profile of v4, /device:TPU:0, one launch (start us, length us, event | category | flops | bytes accessed | tf_op | source)
XLA Modules:
  0.0 34.6 jit_solution(6693068605927256323)
XLA Ops:
  0.6 32.9 %shard_map.84 = (f32[80,4,128]{2,1,0:T(4,128)S(1)}, f32[80,4,128]{2,1,0:T(4,128)S(1)}, f32[80,4,128]{2,1,0:T(4,128)S(1)}, bf16[32,80,128]{2,1,0:T(8,128)(2,1)S(1)}) custom-call(bf16[256,2560]{1,0:T(8,128)(2,1)} %x_hbm.1, bf16[256,512]{1,0:T(8,128)(2,1)} %g_hbm.1, f32[80,4,128]{2,1,0:T(4,128)} %w_hbm.1, f32[80,4,128]{2,1,0:T(4,128)} %m_hbm.1, f32[80,4,128]{2,1,0:T(4,128)} %v_hbm.1), custom_call_target="tpu_custom_call" | custom-call | tf_op jit(solution)/shard_map/pallas_call | solution.py:519
  33.5 1.0 %shard_map.85 = (f32[80,4,128]{2,1,0:T(4,128)}, f32[80,4,128]{2,1,0:T(4,128)}, f32[80,4,128]{2,1,0:T(4,128)}, bf16[1,2560,128]{2,1,0:T(8,128)(2,1)}) custom-call(f32[80,4,128]{2,1,0:T(4,128)S(1)} %get-tuple-element.8.refs_0_, f32[80,4,128]{2,1,0:T(4,128)S(1)} %get-tuple-element.9.refs_1_, f32[80,4,128]{2,1,0:T(4,128)S(1)} %get-tuple-element.10.refs_2_, ...), custom_call_target="tpu_custom_call" | custom-call | tf_op jit(solution)/shard_map/pallas_call | solution.py:567

commit v5 on v4

--- a/solution.py
+++ b/solution.py
@@ -102,13 +102,13 @@
     load_g = pltpu.make_async_copy(g_hbm, g_ref, load_sem.at[0])
     load_x = [
         pltpu.make_async_copy(
-            x_hbm.at[:, columns(*place)], x_ref.at[:, columns(*place)], load_sem.at[4 + i]
+            x_hbm.at[:, columns(*place)], x_ref.at[:, columns(*place)], load_sem.at[2 + i]
         )
         for i, place in enumerate(tiles)
     ]
     load_state = [
-        pltpu.make_async_copy(source, target, load_sem.at[1 + i])
-        for i, (source, target) in enumerate(((w_hbm, w_ref), (m_hbm, m_ref), (v_hbm, v_ref)))
+        pltpu.make_async_copy(source, target, load_sem.at[1])
+        for source, target in ((w_hbm, w_ref), (m_hbm, m_ref), (v_hbm, v_ref))
     ]
     load_g.start()
     for load in load_x + load_state:
@@ -474,7 +474,7 @@
 ORDER = (
     ("join", 0), ("join", 1), ("join", 2), ("point", 1), ("point", 2), ("point", 3),
     ("join", 4), ("second", 0), ("join", 3), ("second", 1), ("second", 2), ("column", 0),
-    ("second", 3), ("across", 4), ("column", 1), ("column", 2), ("update", 0), ("column", 3),
+    ("second", 3), ("column", 1), ("across", 4), ("column", 2), ("update", 0), ("column", 3),
     ("update", 1), ("near", 0), ("update", 4), ("gate", 0), ("update", 2), ("near", 1),
     ("update", 3), ("gate", 1), ("near", 4), ("gate", 4), ("end", 0), ("near", 2), ("gate", 2),
     ("near", 3), ("gate", 3), ("end", 1), ("end", 4), ("end", 2), ("end", 3),
@@ -541,14 +541,14 @@
             pltpu.VMEM((2, 2, pieces[-1][1], width), narrow),
             pltpu.VMEM((3, pieces[-1][1], width), narrow),
             pltpu.VMEM((heads, rows, head_size), narrow),
-            dma((4 + 2 * layers,)),
+            dma((2 + 2 * layers,)),
             dma,
             dma((layers * len(pieces),)),
             dma,
-            dma((layers * len(pieces),)),
-            dma((layers * len(pieces),)),
-            dma,
-            dma((len(pieces),)),
+            dma((layers * (len(pieces) - 1),)),
+            dma((layers * (len(pieces) - 1),)),
+            dma,
+            dma((len(pieces) - 1,)),
             dma,
             dma((depth * len(pieces),)),
             dma,

time: 34.7 us -> 34.4 us (level)
    pallas_call x1, Pallas kernels: 32.9 us -> 32.5 us  [fused(): pl.pallas_call(functools.partial(step_kernel, n, pieces), out_shape=tuple...]
where the time goes in v5:
time: 34.4 us; the launch traced here: 34.2 us
  Pallas kernels  33.6 us (98%)
  between operations  0.64 us (2%)
    pallas_call x1, Pallas kernels, fused(): pl.pallas_call(functools.partial(step_kernel, n, pieces), out_shape=tuple...  32.5 us
    pallas_call x1, Pallas kernels, fused(): pl.pallas_call(finish_kernel, out_shape=(state, state, state, block), in_...  1.04 us

profile of v5, /device:TPU:0, one launch (start us, length us, event | category | flops | bytes accessed | tf_op | source)
XLA Modules:
  0.0 34.2 jit_solution(2516393962642076712)
XLA Ops:
  0.6 32.5 %shard_map.84 = (f32[80,4,128]{2,1,0:T(4,128)S(1)}, f32[80,4,128]{2,1,0:T(4,128)S(1)}, f32[80,4,128]{2,1,0:T(4,128)S(1)}, bf16[32,80,128]{2,1,0:T(8,128)(2,1)S(1)}) custom-call(bf16[256,2560]{1,0:T(8,128)(2,1)} %x_hbm.1, bf16[256,512]{1,0:T(8,128)(2,1)} %g_hbm.1, f32[80,4,128]{2,1,0:T(4,128)} %w_hbm.1, f32[80,4,128]{2,1,0:T(4,128)} %m_hbm.1, f32[80,4,128]{2,1,0:T(4,128)} %v_hbm.1), custom_call_target="tpu_custom_call" | custom-call | tf_op jit(solution)/shard_map/pallas_call | solution.py:519
  33.2 1.0 %shard_map.85 = (f32[80,4,128]{2,1,0:T(4,128)}, f32[80,4,128]{2,1,0:T(4,128)}, f32[80,4,128]{2,1,0:T(4,128)}, bf16[1,2560,128]{2,1,0:T(8,128)(2,1)}) custom-call(f32[80,4,128]{2,1,0:T(4,128)S(1)} %get-tuple-element.8.refs_0_, f32[80,4,128]{2,1,0:T(4,128)S(1)} %get-tuple-element.9.refs_1_, f32[80,4,128]{2,1,0:T(4,128)S(1)} %get-tuple-element.10.refs_2_, ...), custom_call_target="tpu_custom_call" | custom-call | tf_op jit(solution)/shard_map/pallas_call | solution.py:567

commit v6 on v5

--- a/solution.py
+++ b/solution.py
@@ -398,7 +398,7 @@
                 )
             point(0)
         mate_copy(0, t).start()
-    for k in range(1, len(pieces)):
+    for k in (1, len(pieces) - 1, *range(2, len(pieces) - 1)):
         for t in range(layers):
             mate_copy(k, t).start()
     for t in range(layers):

time: 34.4 us -> 34.4 us (level)
  no operation moved by 1% of the time
where the time goes in v6:
time: 34.4 us; the launch traced here: 34.3 us
  Pallas kernels  33.6 us (98%)
  between operations  0.64 us (2%)
    pallas_call x1, Pallas kernels, fused(): pl.pallas_call(functools.partial(step_kernel, n, pieces), out_shape=tuple...  32.6 us
    pallas_call x1, Pallas kernels, fused(): pl.pallas_call(finish_kernel, out_shape=(state, state, state, block), in_...  1.04 us

profile of v6, /device:TPU:0, one launch (start us, length us, event | category | flops | bytes accessed | tf_op | source)
XLA Modules:
  0.0 34.3 jit_solution(11648198794051822183)
XLA Ops:
  0.6 32.6 %shard_map.84 = (f32[80,4,128]{2,1,0:T(4,128)S(1)}, f32[80,4,128]{2,1,0:T(4,128)S(1)}, f32[80,4,128]{2,1,0:T(4,128)S(1)}, bf16[32,80,128]{2,1,0:T(8,128)(2,1)S(1)}) custom-call(bf16[256,2560]{1,0:T(8,128)(2,1)} %x_hbm.1, bf16[256,512]{1,0:T(8,128)(2,1)} %g_hbm.1, f32[80,4,128]{2,1,0:T(4,128)} %w_hbm.1, f32[80,4,128]{2,1,0:T(4,128)} %m_hbm.1, f32[80,4,128]{2,1,0:T(4,128)} %v_hbm.1), custom_call_target="tpu_custom_call" | custom-call | tf_op jit(solution)/shard_map/pallas_call | solution.py:519
  33.2 1.0 %shard_map.85 = (f32[80,4,128]{2,1,0:T(4,128)}, f32[80,4,128]{2,1,0:T(4,128)}, f32[80,4,128]{2,1,0:T(4,128)}, bf16[1,2560,128]{2,1,0:T(8,128)(2,1)}) custom-call(f32[80,4,128]{2,1,0:T(4,128)S(1)} %get-tuple-element.8.refs_0_, f32[80,4,128]{2,1,0:T(4,128)S(1)} %get-tuple-element.9.refs_1_, f32[80,4,128]{2,1,0:T(4,128)S(1)} %get-tuple-element.10.refs_2_, ...), custom_call_target="tpu_custom_call" | custom-call | tf_op jit(solution)/shard_map/pallas_call | solution.py:567
